TPU v7x, 32 devices: a whole 2x2x4 slice. The times are simulated.
32 devices in a mesh: mode: 4 (over y, x), mesh: 8 (over z, core).
Axes of the slice: x: 2, y: 2, z: 4, core: 2. Of those that a mesh axis runs over, the one named last changes fastest.
Arguments:
- velocity: float32 [3, 2, 64, 20480], P(None, None, 'mode', 'mesh'), may hold values from -2.1 to 2.1
- magnetic: float32 [3, 2, 64, 20480], P(None, None, 'mode', 'mesh'), may hold values from -2.1 to 2.1
- leaf_inverse: bfloat16 [64, 160, 128, 128], P('mode', 'mesh'), may hold values from -1 to 2
- leaf_coupling: bfloat16 [64, 128, 20480], P('mode', None, 'mesh'), may hold values from -0.05908203 to 0.05908203
- separator_inverse: bfloat16 [64, 1024, 128], P('mode', 'mesh'), may hold values from -1 to 2
- separator_coupling: bfloat16 [64, 1024, 128], P('mode', 'mesh'), may hold values from -0.26367188 to 0.26367188
- separator_source: float32 [2, 64, 1024], P(None, 'mode', 'mesh'), may hold values from -6 to 6
- front_rows: int32 [8, 2, 128], P('mesh'), may hold values from 0 to 127, each once within a row
Outputs:
- nonlinear: float32 [3, 2, 64, 20480], P(None, None, 'mode', 'mesh')
- azimuthal_field: float32 [2, 64, 20480], P(None, 'mode', 'mesh')
- separator_solution: float32 [2, 64, 1024], P(None, 'mode', 'mesh')
Inputs may be any that keep to these rules, and one draw needn't show every extreme that they name: front_rows[p, 0] and front_rows[p, 1] each hold every number below 128 once.
All inputs are finite; a program needn't handle non-finite values.
Results may differ from a plain program's by a relative error of at most 0.015.
Values may be sent and summed in bfloat16 or wider, within the bound.
No kernel may reach another device: no remote copies, remote signals or barrier semaphores. Data moves between devices by JAX's collectives and lax.ppermute only.
A program may use at most 128 MiB of HBM per device.

v0:
```python
import jax
import jax.numpy as jnp
from jax import lax
from jax.sharding import PartitionSpec as P

M = 64
NPHI = 192
highest = lax.Precision.HIGHEST
dt_step = 0.5


def tables():
    angles = jnp.arange(NPHI, dtype=jnp.int32)[:, None]
    orders = jnp.arange(M, dtype=jnp.int32)[None, :]
    phase = (angles * orders % NPHI).astype(jnp.float32) * (2.0 * jnp.pi / NPHI)
    forward = jnp.stack([jnp.cos(phase), jnp.sin(phase)], axis=1)
    weights = jnp.where(orders == 0, 1.0, 2.0).astype(jnp.float32) / NPHI
    backward = jnp.stack([(jnp.cos(phase) * weights).T, (jnp.sin(phase) * weights).T], axis=0)
    return (forward, backward)


def cross_terms(first, second):
    return jnp.stack(
        [
            first[1] * second[2] - first[2] * second[1],
            first[2] * second[0] - first[0] * second[2],
            first[0] * second[1] - first[1] * second[0],
        ]
    )


def forward_fields(forward, velocity, magnetic):
    return (
        jnp.einsum("kam,camn->ckn", forward, velocity, precision=highest),
        jnp.einsum("kam,camn->ckn", forward, magnetic, precision=highest),
    )


def gather_children(values):
    return lax.all_gather(values, "mesh", axis=2, tiled=True)


def gather_parents(values):
    return lax.all_gather(values, "mesh", axis=2, tiled=True)


def block_of(whole, index, partitions, sep_rows):
    start = (jnp.clip(index, 0, partitions - 1) * sep_rows).astype(jnp.int32)
    return lax.dynamic_slice_in_dim(whole, start, sep_rows, 2)


def shards(
    velocity,
    magnetic,
    leaf_inverse,
    leaf_coupling,
    separator_inverse,
    separator_coupling,
    separator_source,
    front_rows,
):
    modes_dev = velocity.shape[2]
    nodes_dev = velocity.shape[3]
    forward, backward = tables()
    spread_velocity, spread_magnetic = (
        lax.all_to_all(
            velocity.astype(jnp.bfloat16), "mode", split_axis=3, concat_axis=2, tiled=True
        ).astype(velocity.dtype),
        lax.all_to_all(
            magnetic.astype(jnp.bfloat16), "mode", split_axis=3, concat_axis=2, tiled=True
        ).astype(magnetic.dtype),
    )
    phys_velocity, phys_magnetic = forward_fields(forward, spread_velocity, spread_magnetic)
    local_terms = jnp.einsum(
        "amk,ckn->camn", backward, cross_terms(phys_velocity, phys_magnetic), precision=highest
    )
    nonlinear = lax.all_to_all(
        local_terms.astype(jnp.bfloat16), "mode", split_axis=2, concat_axis=3, tiled=True
    ).astype(local_terms.dtype)
    blocks_dev = leaf_inverse.shape[1]
    block_width = leaf_inverse.shape[2]
    sep_rows = separator_source.shape[2]
    source = (magnetic[1] + dt_step * nonlinear[1]).astype(jnp.bfloat16)
    leaf_solved = (
        jnp.einsum(
            "mkij,cmkj->cmki",
            leaf_inverse,
            source.reshape(2, modes_dev, blocks_dev, block_width),
            preferred_element_type=jnp.float32,
        )
        .reshape(2, modes_dev, nodes_dev)
        .astype(jnp.bfloat16)
    )
    row_order = front_rows[0]
    leaf_map = jnp.take(leaf_coupling, row_order[0], axis=1)
    upward_map = jnp.take(separator_coupling, row_order[1], axis=1)
    leaf_update = jnp.einsum(
        "mij,cmj->cmi", leaf_map, leaf_solved, preferred_element_type=jnp.float32
    )
    partitions = lax.axis_size("mesh")
    levels = partitions.bit_length() - 1
    position = lax.axis_index("mesh")
    depth_now = sum(
        [(position % 2**bit_now == 0).astype(jnp.int32) for bit_now in range(1, levels + 1)]
    )
    level_here = depth_now + 1

    def settle(arrived, height, reduced, outgoing):
        fresh = jnp.einsum(
            "mij,cmj->cmi",
            separator_inverse,
            (separator_source - arrived).astype(jnp.bfloat16),
            preferred_element_type=jnp.float32,
        ).astype(jnp.bfloat16)
        sending = jnp.einsum("mij,cmj->cmi", upward_map, fresh, preferred_element_type=jnp.float32)
        active = level_here == height
        return (jnp.where(active, fresh, reduced), jnp.where(active, sending, outgoing))

    reduced = jnp.zeros(separator_source.shape, jnp.bfloat16)
    outgoing = jnp.zeros(separator_source.shape, jnp.float32)
    everyone = gather_children(leaf_update)
    arrived = block_of(everyone, position - 1, partitions, sep_rows) + block_of(
        everyone, position, partitions, sep_rows
    )
    reduced, outgoing = settle(arrived, 1, reduced, outgoing)
    for height in range(2, levels + 1):
        gap = 2 ** (height - 2)
        everyone = gather_children(outgoing)
        arrived = block_of(everyone, position - gap, partitions, sep_rows) + block_of(
            everyone, position + gap, partitions, sep_rows
        )
        reduced, outgoing = settle(arrived, height, reduced, outgoing)
    everyone = gather_children(outgoing)
    reduced, outgoing = settle(
        block_of(everyone, partitions // 2, partitions, sep_rows), levels + 1, reduced, outgoing
    )
    top_value = jnp.einsum(
        "mij,cmi->cmj", separator_inverse, reduced, preferred_element_type=jnp.float32
    )
    solution = jnp.where(
        level_here == levels + 1, top_value, jnp.zeros(separator_source.shape, jnp.float32)
    )
    for height in range(levels, 0, -1):
        everyone = gather_parents(solution.astype(jnp.bfloat16))
        if height == levels:
            parent = position * 0
        else:
            parent = position // 2 ** (height + 1) * 2 ** (height + 1) + 2**height
        above = block_of(everyone, parent, partitions, sep_rows)
        residue = reduced.astype(jnp.float32) - jnp.einsum(
            "mij,cmi->cmj", upward_map, above, preferred_element_type=jnp.float32
        )
        fresh = jnp.einsum(
            "mij,cmi->cmj",
            separator_inverse,
            residue.astype(jnp.bfloat16),
            preferred_element_type=jnp.float32,
        )
        solution = jnp.where(level_here == height, fresh, solution)
    everyone = gather_parents(solution.astype(jnp.bfloat16))
    above = block_of(everyone, 2 * (position // 2) + 1, partitions, sep_rows)
    residue = leaf_solved.astype(jnp.float32) - jnp.einsum(
        "mij,cmi->cmj", leaf_map, above, preferred_element_type=jnp.float32
    )
    azimuthal_field = jnp.einsum(
        "mkji,cmkj->cmki",
        leaf_inverse,
        residue.astype(jnp.bfloat16).reshape(2, modes_dev, blocks_dev, block_width),
        preferred_element_type=jnp.float32,
    ).reshape(2, modes_dev, nodes_dev)
    return (nonlinear, azimuthal_field, solution)


def solution(mesh):
    in_specs = (
        P(None, None, "mode", "mesh"),
        P(None, None, "mode", "mesh"),
        P("mode", "mesh", None, None),
        P("mode", None, "mesh"),
        P("mode", "mesh", None),
        P("mode", "mesh", None),
        P(None, "mode", "mesh"),
        P("mesh", None, None),
    )
    out_specs = (P(None, None, "mode", "mesh"), P(None, "mode", "mesh"), P(None, "mode", "mesh"))
    return jax.shard_map(shards, mesh=mesh, in_specs=in_specs, out_specs=out_specs, check_vma=False)
```

profile of v0, /device:TPU:0, one launch (start us, length us, event | category | flops | bytes accessed | tf_op | source)
XLA Modules:
  0.0 205.2 jit_solution(15129035748217924793)
XLA Ops:
  2.0 5.2 %copy.84 = bf16[3,2,16,2560]{2,0,1,3:T(4,128)(2,1)} copy(bf16[3,2,16,2560]{3,2,1,0:T(8,128)(2,1)S(1)} %convert_element_type.163) | data formatting | bytes 983040 | tf_op jit(solution)/shard_map/convert_element_type | solution.py:70
  7.2 6.7 %reshape.281 = bf16[4,2,30720]{2,1,0:T(2,128)(2,1)} reshape(bf16[2560,2,3,16]{3,2,1,0:T(4,128)(2,1)} %bitcast.190) | data formatting | bytes 983040
  13.9 5.2 %all-to-all-start.1 = ((bf16[4,2,30720]{2,1,0:T(2,128)(2,1)}), bf16[4,2,30720]{2,1,0:T(2,128)(2,1)S(1)}, u32[]{:S(2)}, u32[]{:S(2)}) async-start(bf16[4,2,30720]{2,1,0:T(2,128)(2,1)} %reshape.281), calls=%async_computation.1 | async-start | bytes 983040 | tf_op jit(solution)/shard_map/all_to_all | solution.py:69
  19.1 5.2 %copy.82 = bf16[3,2,16,2560]{2,0,1,3:T(4,128)(2,1)} copy(bf16[3,2,16,2560]{3,2,1,0:T(8,128)(2,1)S(1)} %convert_element_type.162) | data formatting | bytes 983040 | tf_op jit(solution)/shard_map/convert_element_type | solution.py:67
  24.3 6.7 %reshape.279 = bf16[4,2,30720]{2,1,0:T(2,128)(2,1)} reshape(bf16[2560,2,3,16]{3,2,1,0:T(4,128)(2,1)} %bitcast.191) | data formatting | bytes 983040
  31.0 4.2 %all-to-all-start = ((bf16[4,2,30720]{2,1,0:T(2,128)(2,1)}), bf16[4,2,30720]{2,1,0:T(2,128)(2,1)S(1)}, u32[]{:S(2)}, u32[]{:S(2)}) async-start(bf16[4,2,30720]{2,1,0:T(2,128)(2,1)} %reshape.279), calls=%async_computation | async-start | bytes 983040 | tf_op jit(solution)/shard_map/all_to_all | solution.py:66
  35.8 6.0 %reshape.282 = bf16[2560,2,3,16]{3,2,1,0:T(4,128)(2,1)} reshape(bf16[4,2,30720]{2,1,0:T(2,128)(2,1)S(1)} %all-to-all-done.1) | data formatting | bytes 983040
  41.8 5.8 %copy.85 = bf16[3,2,16,4,640]{4,2,3,1,0:T(8,128)(2,1)S(1)} copy(bf16[3,2,16,4,640]{2,0,1,4,3:T(4,128)(2,1)} %bitcast.192) | data formatting | bytes 983040 | tf_op jit(solution)/shard_map/all_to_all | solution.py:69
  47.5 6.0 %reshape.280 = bf16[2560,2,3,16]{3,2,1,0:T(4,128)(2,1)} reshape(bf16[4,2,30720]{2,1,0:T(2,128)(2,1)S(1)} %all-to-all-done) | data formatting | bytes 983040
  53.5 5.8 %copy.83 = bf16[3,2,16,4,640]{4,2,3,1,0:T(8,128)(2,1)S(1)} copy(bf16[3,2,16,4,640]{2,0,1,4,3:T(4,128)(2,1)} %bitcast.193) | data formatting | bytes 983040 | tf_op jit(solution)/shard_map/all_to_all | solution.py:66
  63.5 4.2 %all-to-all-start.2 = ((bf16[3,2,64,640]{3,1,0,2:T(2,128)(2,1)}), bf16[3,2,64,640]{3,1,0,2:T(2,128)(2,1)S(1)}, u32[]{:S(2)}, u32[]{:S(2)}) async-start(bf16[3,2,64,640]{3,1,0,2:T(2,128)(2,1)} %copy.86), calls=%async_computation.2 | async-start | bytes 983040 | tf_op jit(solution)/shard_map/all_to_all | solution.py:77
  67.9 2.8 %gather_fusion.1 = bf16[128,16,128]{2,0,1:T(8,128)(2,1)S(1)} fusion(bf16[16,128,128]{2,1,0:T(8,128)(2,1)S(1)} %copy-done, s32[1024]{0:T(1024)S(1)} %pad_clamp_fusion), kind=kCustom, calls=%fused_computation.1 | custom fusion | bytes 1049088 | tf_op jit(solution)/shard_map/jit(_take)/gather | solution.py:96
  70.6 24.7 %gather_fusion = bf16[128,16,2560]{2,0,1:T(8,128)(2,1)} fusion(bf16[16,128,2560]{2,1,0:T(8,128)(2,1)} %param.11, s32[1024]{0:T(1024)S(1)} %pad_clamp_fusion.1), kind=kCustom, calls=%fused_computation | custom fusion | bytes 20972032 | tf_op jit(solution)/shard_map/jit(_take)/gather | solution.py:95
  97.6 9.0 %fusion.20 = bf16[2,16,2560]{2,0,1:T(2,128)(2,1)S(1)} fusion(bf16[16,20,128,128]{3,2,1,0:T(8,128)(2,1)} %param.10, bf16[2,16,20,128]{3,2,1,0:T(8,128)(2,1)S(1)} %convert_element_type.172), kind=kOutput, calls=%fused_computation.22 | convolution fusion | flops 21053440 | bytes 10813440 | tf_op jit(solution)/shard_map/mkij,cmkj->cmki/dot_general | solution.py:85
  106.7 2.9 %fusion.26 = f32[2,16,128]{2,0,1:T(2,128)S(1)} fusion(bf16[2,16,2560]{2,0,1:T(2,128)(2,1)S(1)} %fusion.20, bf16[128,16,2560]{2,0,1:T(8,128)(2,1)S(1)} %copy-done.2, pred[128]{0:T(512)(128)(4,1)S(1)} %get-tuple-element.25), kind=kOutput, calls=%fused_computation.24 | convolution fusion | flops 26214400 | bytes 10666112 | tf_op jit(solution)/shard_map/mij,cmj->cmi/dot_general | solution.py:97
  109.5 12.5 %all_gather.24 = f32[2,16,1024]{2,0,1:T(2,128)S(1)} all-gather(f32[2,16,128]{2,0,1:T(2,128)S(1)} %fusion.26), channel_id=1, replica_groups=mesh['mode'=4,'mesh'=8] {'mesh'}, dimensions={2}, use_global_device_ids=true | all-gather | bytes 147456 | tf_op jit(solution)/shard_map/all_gather | solution.py:40
  122.9 9.3 %all_gather.25 = f32[2,16,1024]{2,0,1:T(2,128)S(1)} all-gather(f32[2,16,128]{2,0,1:T(2,128)S(1)} %fusion.35), channel_id=1, replica_groups=mesh['mode'=4,'mesh'=8] {'mesh'}, dimensions={2}, use_global_device_ids=true | all-gather | bytes 147456 | tf_op jit(solution)/shard_map/all_gather | solution.py:40
  133.0 10.6 %all_gather.26 = f32[2,16,1024]{2,0,1:T(2,128)S(1)} all-gather(f32[2,16,128]{2,0,1:T(2,128)S(1)} %fusion.34), channel_id=1, replica_groups=mesh['mode'=4,'mesh'=8] {'mesh'}, dimensions={2}, use_global_device_ids=true | all-gather | bytes 147456 | tf_op jit(solution)/shard_map/all_gather | solution.py:40
  144.4 9.3 %all_gather.27 = f32[2,16,1024]{2,0,1:T(2,128)S(1)} all-gather(f32[2,16,128]{2,0,1:T(2,128)S(1)} %fusion.33), channel_id=1, replica_groups=mesh['mode'=4,'mesh'=8] {'mesh'}, dimensions={2}, use_global_device_ids=true | all-gather | bytes 147456 | tf_op jit(solution)/shard_map/all_gather | solution.py:40
  154.3 10.3 %all_gather.28 = bf16[2,16,1024]{2,0,1:T(2,128)(2,1)S(1)} all-gather(bf16[2,16,128]{2,0,1:T(2,128)(2,1)S(1)} %convert_bitcast_fusion.2), channel_id=1, replica_groups=mesh['mode'=4,'mesh'=8] {'mesh'}, dimensions={2}, use_global_device_ids=true | all-gather | bytes 73728 | tf_op jit(solution)/shard_map/all_gather | solution.py:44
  165.1 9.0 %all_gather.29 = bf16[2,16,1024]{2,0,1:T(2,128)(2,1)S(1)} all-gather(bf16[2,16,128]{2,0,1:T(2,128)(2,1)S(1)} %convert_bitcast_fusion.1), channel_id=1, replica_groups=mesh['mode'=4,'mesh'=8] {'mesh'}, dimensions={2}, use_global_device_ids=true | all-gather | bytes 73728 | tf_op jit(solution)/shard_map/all_gather | solution.py:44
  174.6 10.3 %all_gather.30 = bf16[2,16,1024]{2,0,1:T(2,128)(2,1)S(1)} all-gather(bf16[2,16,128]{2,0,1:T(2,128)(2,1)S(1)} %convert_bitcast_fusion), channel_id=1, replica_groups=mesh['mode'=4,'mesh'=8] {'mesh'}, dimensions={2}, use_global_device_ids=true | all-gather | bytes 73728 | tf_op jit(solution)/shard_map/all_gather | solution.py:44
  186.0 9.1 %all_gather.31 = bf16[2,16,1024]{2,0,1:T(2,128)(2,1)S(1)} all-gather(bf16[2,16,128]{2,0,1:T(2,128)(2,1)S(1)} %get-tuple-element.30), channel_id=1, replica_groups=mesh['mode'=4,'mesh'=8] {'mesh'}, dimensions={2}, use_global_device_ids=true | all-gather | bytes 73728 | tf_op jit(solution)/shard_map/all_gather | solution.py:44
  195.1 9.3 %convolution_bitcast_fusion.2 = f32[2,16,20,128]{3,0,2,1:T(2,128)S(1)} fusion(bf16[16,20,128,128]{3,2,1,0:T(8,128)(2,1)} %param.10, bf16[128,16,2560]{2,0,1:T(8,128)(2,1)} %gather_fusion, pred[128]{0:T(512)(128)(4,1)S(1)} %get-tuple-element.25, bf16[2,16,2560]{2,0,1:T(2,128)(2,1)S(1)} %fusion.20, bf16[2,16,1024]{2,0,1:T(2,128)(2,1)S(1)} %all_gather.31, ...), kind=kOutput, calls=%fused_computation.20 | convolution fusion | flops 47431680 | bytes 21471748 | tf_op jit(solution)/shard_map/mkji,cmkj->cmki/dot_general | solution.py:165
  (54 shorter events, 14.4 us)
Async XLA Ops:
  0.6 67.2 %copy-start = (bf16[16,128,128]{2,1,0:T(8,128)(2,1)S(1)}, bf16[16,128,128]{2,1,0:T(8,128)(2,1)}, u32[]{:S(2)}) copy-start(bf16[16,128,128]{2,1,0:T(8,128)(2,1)} %param.13) | copy-start | bytes 1572868
  0.6 18.4 %copy-start.4 = (f32[3,2,16,2560]{3,2,1,0:T(8,128)S(1)}, f32[3,2,16,2560]{3,2,1,0:T(8,128)}, u32[]{:S(2)}) copy-start(f32[3,2,16,2560]{3,2,1,0:T(8,128)} %param.8) | copy-start | bytes 2949124
  7.2 23.8 %copy-start.6 = (s32[1,2,128]{2,1,0:T(2,128)S(1)}, s32[1,2,128]{2,1,0:T(2,128)}, u32[]{:S(2)}) copy-start(s32[1,2,128]{2,1,0:T(2,128)} %param.15) | copy-start | bytes 3076
  13.9 17.1 %all-to-all-start.1 = ((bf16[4,2,30720]{2,1,0:T(2,128)(2,1)}), bf16[4,2,30720]{2,1,0:T(2,128)(2,1)S(1)}, u32[]{:S(2)}, u32[]{:S(2)}) async-start(bf16[4,2,30720]{2,1,0:T(2,128)(2,1)} %reshape.281), calls=%async_computation.1 | async-start | bytes 983040 | tf_op jit(solution)/shard_map/all_to_all | solution.py:69
  31.0 16.5 %all-to-all-start = ((bf16[4,2,30720]{2,1,0:T(2,128)(2,1)}), bf16[4,2,30720]{2,1,0:T(2,128)(2,1)S(1)}, u32[]{:S(2)}, u32[]{:S(2)}) async-start(bf16[4,2,30720]{2,1,0:T(2,128)(2,1)} %reshape.279), calls=%async_computation | async-start | bytes 983040 | tf_op jit(solution)/shard_map/all_to_all | solution.py:66
  63.5 31.8 %all-to-all-start.2 = ((bf16[3,2,64,640]{3,1,0,2:T(2,128)(2,1)}), bf16[3,2,64,640]{3,1,0,2:T(2,128)(2,1)S(1)}, u32[]{:S(2)}, u32[]{:S(2)}) async-start(bf16[3,2,64,640]{3,1,0,2:T(2,128)(2,1)} %copy.86), calls=%async_computation.2 | async-start | bytes 983040 | tf_op jit(solution)/shard_map/all_to_all | solution.py:77
  96.6 10.1 %copy-start.2 = (bf16[128,16,2560]{2,0,1:T(8,128)(2,1)S(1)}, bf16[128,16,2560]{2,0,1:T(8,128)(2,1)}, u32[]{:S(2)}) copy-start(bf16[128,16,2560]{2,0,1:T(8,128)(2,1)} %gather_fusion) | copy-start | bytes 31457284
  106.6 15.4 %copy-start.3 = (bf16[16,128,128]{2,1,0:T(8,128)(2,1)S(1)}, bf16[16,128,128]{2,1,0:T(8,128)(2,1)}, u32[]{:S(2)}) copy-start(bf16[16,128,128]{2,1,0:T(8,128)(2,1)} %param.12) | copy-start | bytes 1572868
  106.6 15.4 %copy-start.5 = (f32[2,16,128]{2,1,0:T(8,128)S(1)}, f32[2,16,128]{2,1,0:T(8,128)}, u32[]{:S(2)}) copy-start(f32[2,16,128]{2,1,0:T(8,128)} %param.14) | copy-start | bytes 49156
  186.0 19.3 %copy-start.1 = (bf16[16,128,128]{2,1,0:T(8,128)(2,1)S(1)}, bf16[16,128,128]{2,1,0:T(8,128)(2,1)}, u32[]{:S(2)}) copy-start(bf16[16,128,128]{2,1,0:T(8,128)(2,1)} %param.13) | copy-start | bytes 1572868
where the time goes:
time: 206 us; the launch traced here: 205 us
  blocking collectives  80.5 us (39%)
  local copies, waits for them, and re-layouts  78.6 us (38%)
  matrix products  28.4 us (14%)
  starting transfers between devices  13.6 us (7%)
  other arithmetic  3.23 us (2%)
    all_gather x4, blocking collectives, gather_children(): return lax.all_gather(values, 'mesh', axis=2, tiled=True)  41.7 us
    all_gather x4, blocking collectives, gather_parents(): return lax.all_gather(values, 'mesh', axis=2, tiled=True)  38.7 us
    unnamed x19, local copies, waits for them, and re-layouts  25.9 us
    gather x1, local copies, waits for them, and re-layouts, shards(): leaf_map = jnp.take(leaf_coupling, row_order[0], axis=1)  24.7 us
    dot_general x1, matrix products, shards(): jnp.einsum('mkji,cmkj->cmki', leaf_inverse, residue.astype(jnp.bfloat16)....  9.34 us
    dot_general x1, matrix products, shards(): jnp.einsum('mkij,cmkj->cmki', leaf_inverse, source.reshape(2, modes_dev,...  8.98 us
    all_to_all x1, local copies, waits for them, and re-layouts, shards(): lax.all_to_all(magnetic.astype(jnp.bfloat16), 'mode', split_axis=3, conca...  5.77 us
    all_to_all x1, local copies, waits for them, and re-layouts, shards(): lax.all_to_all(velocity.astype(jnp.bfloat16), 'mode', split_axis=3, conca...  5.77 us
  transfers between devices with their start and end apart: 3, of which 0 were waited for; matrix products, arithmetic and copies ran while one was open for 25% of the time, Pallas kernels for 0%

commit v1 on v0

--- a/solution.py
+++ b/solution.py
@@ -1,12 +1,45 @@
+import functools
 import jax
 import jax.numpy as jnp
 from jax import lax
 from jax.sharding import PartitionSpec as P
+from jax.lax import axis_index, axis_size, ppermute
 
 M = 64
 NPHI = 192
 highest = lax.Precision.HIGHEST
 dt_step = 0.5
+
+
+def finish_page_on(message, out_dim, view):
+    w1 = message.shape
+    return jnp.moveaxis(
+        message.reshape(*w1[:out_dim], view, w1[out_dim] // view, *w1[out_dim + 1 :]), out_dim, 0
+    )
+
+
+def obtain_the_object(local_array, in_dim):
+    local_array = jnp.moveaxis(local_array, 0, in_dim)
+    tile_out = local_array.shape
+    return local_array.reshape(
+        *tile_out[:in_dim], tile_out[in_dim] * tile_out[in_dim + 1], *tile_out[in_dim + 2 :]
+    )
+
+
+def _mark_scales(x0, axis_id, load, q_in):
+    state_now = axis_size(axis_id)
+    block_next, w2 = (state_now, axis_index(axis_id))
+    e_next = finish_page_on(x0, load, block_next)
+    buffers = [e_next[w2]]
+    for no in range(1, block_next):
+        a_next = e_next[w2 ^ no]
+        buffers.append(ppermute(a_next, axis_id, [(s, s ^ no) for s in range(block_next)]))
+    b_next = jnp.stack(buffers, axis=0)
+    e_next = b_next[w2 ^ jnp.arange(block_next)]
+    return obtain_the_object(e_next, q_in)
+
+
+point_lots_all = functools.partial(_mark_scales, axis_id="mode", load=3, q_in=2)
 
 
 def tables():
@@ -66,9 +99,7 @@
         lax.all_to_all(
             velocity.astype(jnp.bfloat16), "mode", split_axis=3, concat_axis=2, tiled=True
         ).astype(velocity.dtype),
-        lax.all_to_all(
-            magnetic.astype(jnp.bfloat16), "mode", split_axis=3, concat_axis=2, tiled=True
-        ).astype(magnetic.dtype),
+        point_lots_all(magnetic.astype(jnp.bfloat16)).astype(magnetic.dtype),
     )
     phys_velocity, phys_magnetic = forward_fields(forward, spread_velocity, spread_magnetic)
     local_terms = jnp.einsum(

time: 206 us -> 189 us (0.917)
  local copies, waits for them, and re-layouts: 78.6 us -> 56.9 us
  waiting for transfers between devices: 0.01 us -> 4.57 us
    unnamed x19 -> x17, local copies, waits for them, and re-layouts: 25.9 us -> 13.3 us
    all_to_all x1 -> x0, local copies, waits for them, and re-layouts: 5.77 us -> none  [shards(): lax.all_to_all(magnetic.astype(jnp.bfloat16), 'mode', split_axis=3, conca...]
    all_to_all x1 -> x0, starting transfers between devices: 5.19 us -> none  [shards(): lax.all_to_all(magnetic.astype(jnp.bfloat16), 'mode', split_axis=3, conca...]
    convert_element_type x1 -> x0, local copies, waits for them, and re-layouts: 5.18 us -> none  [shards(): magnetic.astype(jnp.bfloat16)]
    ppermute x0 -> x3, starting transfers between devices: none -> 4.69 us  [_mark_scales(): ppermute(a_next, axis_id, [(s, s ^ no) for s in range(block_next)])]
    all_to_all x1, waiting for transfers between devices: 0.01 us -> 4.56 us  [shards(): lax.all_to_all(velocity.astype(jnp.bfloat16), 'mode', split_axis=3, conca...]
  transfers between devices with their start and end apart: 3 -> 5, of which waited for: 0 -> 1; matrix products, arithmetic and copies ran while one was open for 25% -> 23% of each run, Pallas kernels for 0% -> 0%
where the time goes in v1:
time: 189 us; the launch traced here: 188 us
  blocking collectives  80.3 us (42%)
  local copies, waits for them, and re-layouts  56.9 us (30%)
  matrix products  28.4 us (15%)
  starting transfers between devices  12.3 us (7%)
  waiting for transfers between devices  4.57 us (2%)
  other arithmetic  4.55 us (2%)
    all_gather x4, blocking collectives, gather_children(): return lax.all_gather(values, 'mesh', axis=2, tiled=True)  41.7 us
    all_gather x4, blocking collectives, gather_parents(): return lax.all_gather(values, 'mesh', axis=2, tiled=True)  38.6 us
    gather x1, local copies, waits for them, and re-layouts, shards(): leaf_map = jnp.take(leaf_coupling, row_order[0], axis=1)  24.7 us
    unnamed x17, local copies, waits for them, and re-layouts  13.3 us
    dot_general x1, matrix products, shards(): jnp.einsum('mkji,cmkj->cmki', leaf_inverse, residue.astype(jnp.bfloat16)....  9.34 us
    dot_general x1, matrix products, shards(): jnp.einsum('mkij,cmkj->cmki', leaf_inverse, source.reshape(2, modes_dev,...  8.98 us
    all_to_all x1, local copies, waits for them, and re-layouts, shards(): lax.all_to_all(velocity.astype(jnp.bfloat16), 'mode', split_axis=3, conca...  5.77 us
    convert_element_type x1, local copies, waits for them, and re-layouts, shards(): velocity.astype(jnp.bfloat16)  5.18 us
  transfers between devices with their start and end apart: 5, of which 1 were waited for; matrix products, arithmetic and copies ran while one was open for 23% of the time, Pallas kernels for 0%

profile of v1, /device:TPU:0, one launch (start us, length us, event | category | flops | bytes accessed | tf_op | source)
XLA Modules:
  0.0 188.1 jit_solution(12196699642407343523)
XLA Ops:
  0.7 1.3 convert_element_type.163
  3.2 3.0 %collective-permute-start = (bf16[3,2,16,640]{3,2,1,0:T(8,128)(2,1)S(1)}, bf16[3,2,16,640]{3,2,1,0:T(8,128)(2,1)S(1)}, u32[]{:S(2)}, u32[]{:S(2)}) collective-permute-start(bf16[3,2,16,640]{3,2,1,0:T(8,128)(2,1)S(1)} %bitcast.217), channel_id=1, source_target_pairs={{0,8},{8,0},{16,24},{24,16},{1,9},{9,1},{17,25},{25,17},{2,10},{10... | collective-permute-start | bytes 368648 | tf_op jit(solution)/shard_map/ppermute | solution.py:36
  6.2 1.6 collective-permute-start.1
  9.2 5.2 %copy.90 = bf16[3,2,16,2560]{2,0,1,3:T(4,128)(2,1)} copy(bf16[3,2,16,2560]{3,2,1,0:T(8,128)(2,1)S(1)} %convert_element_type.162) | data formatting | bytes 983040 | tf_op jit(solution)/shard_map/convert_element_type | solution.py:100
  14.4 6.7 %reshape.318 = bf16[4,2,30720]{2,1,0:T(2,128)(2,1)} reshape(bf16[2560,2,3,16]{3,2,1,0:T(4,128)(2,1)} %bitcast.205) | data formatting | bytes 983040
  21.0 4.2 %all-to-all-start = ((bf16[4,2,30720]{2,1,0:T(2,128)(2,1)}), bf16[4,2,30720]{2,1,0:T(2,128)(2,1)S(1)}, u32[]{:S(2)}, u32[]{:S(2)}) async-start(bf16[4,2,30720]{2,1,0:T(2,128)(2,1)} %reshape.318), calls=%async_computation | async-start | bytes 983040 | tf_op jit(solution)/shard_map/all_to_all | solution.py:99
  27.4 4.6 %all-to-all-done = bf16[4,2,30720]{2,1,0:T(2,128)(2,1)S(1)} async-done(((bf16[4,2,30720]{2,1,0:T(2,128)(2,1)}), bf16[4,2,30720]{2,1,0:T(2,128)(2,1)S(1)}, u32[]{:S(2)}, u32[]{:S(2)}) %all-to-all-start) | async-done | bytes 491552 | tf_op jit(solution)/shard_map/all_to_all | solution.py:99
  32.0 6.0 %reshape.319 = bf16[2560,2,3,16]{3,2,1,0:T(4,128)(2,1)} reshape(bf16[4,2,30720]{2,1,0:T(2,128)(2,1)S(1)} %all-to-all-done) | data formatting | bytes 983040
  38.0 5.8 %copy.91 = bf16[3,2,16,4,640]{4,2,3,1,0:T(8,128)(2,1)S(1)} copy(bf16[3,2,16,4,640]{2,0,1,4,3:T(4,128)(2,1)} %bitcast.206) | data formatting | bytes 983040 | tf_op jit(solution)/shard_map/all_to_all | solution.py:99
  46.0 1.3 copy.93
  47.2 3.5 %all-to-all-start.1 = ((bf16[3,2,64,640]{3,1,0,2:T(2,128)(2,1)}), bf16[3,2,64,640]{3,1,0,2:T(2,128)(2,1)S(1)}, u32[]{:S(2)}, u32[]{:S(2)}) async-start(bf16[3,2,64,640]{3,1,0,2:T(2,128)(2,1)} %copy.93), calls=%async_computation.1 | async-start | bytes 983040 | tf_op jit(solution)/shard_map/all_to_all | solution.py:108
  50.9 2.8 %gather_fusion.2 = bf16[128,16,128]{2,0,1:T(8,128)(2,1)S(1)} fusion(bf16[16,128,128]{2,1,0:T(8,128)(2,1)S(1)} %copy-done, s32[1024]{0:T(1024)S(1)} %pad_clamp_fusion), kind=kCustom, calls=%fused_computation.2 | custom fusion | bytes 1049088 | tf_op jit(solution)/shard_map/jit(_take)/gather | solution.py:127
  53.6 24.7 %gather_fusion.1 = bf16[128,16,2560]{2,0,1:T(8,128)(2,1)} fusion(bf16[16,128,2560]{2,1,0:T(8,128)(2,1)} %param.11, s32[1024]{0:T(1024)S(1)} %pad_clamp_fusion.1), kind=kCustom, calls=%fused_computation.1 | custom fusion | bytes 20972032 | tf_op jit(solution)/shard_map/jit(_take)/gather | solution.py:126
  80.6 9.0 %fusion.20 = bf16[2,16,2560]{2,0,1:T(2,128)(2,1)S(1)} fusion(bf16[16,20,128,128]{3,2,1,0:T(8,128)(2,1)} %param.10, bf16[2,16,20,128]{3,2,1,0:T(8,128)(2,1)S(1)} %convert_element_type.172), kind=kOutput, calls=%fused_computation.23 | convolution fusion | flops 21053440 | bytes 10813440 | tf_op jit(solution)/shard_map/mkij,cmkj->cmki/dot_general | solution.py:116
  89.7 2.9 %fusion.26 = f32[2,16,128]{2,0,1:T(2,128)S(1)} fusion(bf16[2,16,2560]{2,0,1:T(2,128)(2,1)S(1)} %fusion.20, bf16[128,16,2560]{2,0,1:T(8,128)(2,1)S(1)} %copy-done.1, pred[128]{0:T(512)(128)(4,1)S(1)} %get-tuple-element.32), kind=kOutput, calls=%fused_computation.25 | convolution fusion | flops 26214400 | bytes 10666112 | tf_op jit(solution)/shard_map/mij,cmj->cmi/dot_general | solution.py:128
  92.5 12.5 %all_gather.24 = f32[2,16,1024]{2,0,1:T(2,128)S(1)} all-gather(f32[2,16,128]{2,0,1:T(2,128)S(1)} %fusion.26), channel_id=1, replica_groups=mesh['mode'=4,'mesh'=8] {'mesh'}, dimensions={2}, use_global_device_ids=true | all-gather | bytes 147456 | tf_op jit(solution)/shard_map/all_gather | solution.py:73
  105.9 9.3 %all_gather.25 = f32[2,16,1024]{2,0,1:T(2,128)S(1)} all-gather(f32[2,16,128]{2,0,1:T(2,128)S(1)} %fusion.35), channel_id=1, replica_groups=mesh['mode'=4,'mesh'=8] {'mesh'}, dimensions={2}, use_global_device_ids=true | all-gather | bytes 147456 | tf_op jit(solution)/shard_map/all_gather | solution.py:73
  116.0 10.6 %all_gather.26 = f32[2,16,1024]{2,0,1:T(2,128)S(1)} all-gather(f32[2,16,128]{2,0,1:T(2,128)S(1)} %fusion.34), channel_id=1, replica_groups=mesh['mode'=4,'mesh'=8] {'mesh'}, dimensions={2}, use_global_device_ids=true | all-gather | bytes 147456 | tf_op jit(solution)/shard_map/all_gather | solution.py:73
  127.4 9.3 %all_gather.27 = f32[2,16,1024]{2,0,1:T(2,128)S(1)} all-gather(f32[2,16,128]{2,0,1:T(2,128)S(1)} %fusion.33), channel_id=1, replica_groups=mesh['mode'=4,'mesh'=8] {'mesh'}, dimensions={2}, use_global_device_ids=true | all-gather | bytes 147456 | tf_op jit(solution)/shard_map/all_gather | solution.py:73
  137.3 10.3 %all_gather.28 = bf16[2,16,1024]{2,0,1:T(2,128)(2,1)S(1)} all-gather(bf16[2,16,128]{2,0,1:T(2,128)(2,1)S(1)} %convert_bitcast_fusion.2), channel_id=1, replica_groups=mesh['mode'=4,'mesh'=8] {'mesh'}, dimensions={2}, use_global_device_ids=true | all-gather | bytes 73728 | tf_op jit(solution)/shard_map/all_gather | solution.py:77
  148.1 9.0 %all_gather.29 = bf16[2,16,1024]{2,0,1:T(2,128)(2,1)S(1)} all-gather(bf16[2,16,128]{2,0,1:T(2,128)(2,1)S(1)} %convert_bitcast_fusion.1), channel_id=1, replica_groups=mesh['mode'=4,'mesh'=8] {'mesh'}, dimensions={2}, use_global_device_ids=true | all-gather | bytes 73728 | tf_op jit(solution)/shard_map/all_gather | solution.py:77
  157.6 10.3 %all_gather.30 = bf16[2,16,1024]{2,0,1:T(2,128)(2,1)S(1)} all-gather(bf16[2,16,128]{2,0,1:T(2,128)(2,1)S(1)} %convert_bitcast_fusion), channel_id=1, replica_groups=mesh['mode'=4,'mesh'=8] {'mesh'}, dimensions={2}, use_global_device_ids=true | all-gather | bytes 73728 | tf_op jit(solution)/shard_map/all_gather | solution.py:77
  169.0 9.0 %all_gather.31 = bf16[2,16,1024]{2,0,1:T(2,128)(2,1)S(1)} all-gather(bf16[2,16,128]{2,0,1:T(2,128)(2,1)S(1)} %get-tuple-element.37), channel_id=1, replica_groups=mesh['mode'=4,'mesh'=8] {'mesh'}, dimensions={2}, use_global_device_ids=true | all-gather | bytes 73728 | tf_op jit(solution)/shard_map/all_gather | solution.py:77
  177.9 9.3 %convolution_bitcast_fusion.2 = f32[2,16,20,128]{3,0,2,1:T(2,128)S(1)} fusion(bf16[16,20,128,128]{3,2,1,0:T(8,128)(2,1)} %param.10, bf16[128,16,2560]{2,0,1:T(8,128)(2,1)} %gather_fusion.1, pred[128]{0:T(512)(128)(4,1)S(1)} %get-tuple-element.32, bf16[2,16,2560]{2,0,1:T(2,128)(2,1)S(1)} %fusion.20, bf16[2,16,1024]{2,0,1:T(2,128)(2,1)S(1)} %all_gather.31, ...), kind=kOutput, calls=%fused_computation.21 | convolution fusion | flops 47431680 | bytes 21471748 | tf_op jit(solution)/shard_map/mkji,cmkj->cmki/dot_general | solution.py:196
  (61 shorter events, 15.1 us)
Async XLA Ops:
  0.6 50.2 %copy-start = (bf16[16,128,128]{2,1,0:T(8,128)(2,1)S(1)}, bf16[16,128,128]{2,1,0:T(8,128)(2,1)}, u32[]{:S(2)}) copy-start(bf16[16,128,128]{2,1,0:T(8,128)(2,1)} %param.13) | copy-start | bytes 1572868
  0.6 24.8 %copy-start.4 = (s32[1,2,128]{2,1,0:T(2,128)S(1)}, s32[1,2,128]{2,1,0:T(2,128)}, u32[]{:S(2)}) copy-start(s32[1,2,128]{2,1,0:T(2,128)} %param.15) | copy-start | bytes 3076
  3.2 22.7 %collective-permute-start = (bf16[3,2,16,640]{3,2,1,0:T(8,128)(2,1)S(1)}, bf16[3,2,16,640]{3,2,1,0:T(8,128)(2,1)S(1)}, u32[]{:S(2)}, u32[]{:S(2)}) collective-permute-start(bf16[3,2,16,640]{3,2,1,0:T(8,128)(2,1)S(1)} %bitcast.217), channel_id=1, source_target_pairs={{0,8},{8,0},{16,24},{24,16},{1,9},{9,1},{17,25},{25,17},{2,10},{10... | collective-permute-start | bytes 368648 | tf_op jit(solution)/shard_map/ppermute | solution.py:36
  6.2 19.6 %collective-permute-start.1 = (bf16[3,2,16,640]{3,2,1,0:T(8,128)(2,1)S(1)}, bf16[3,2,16,640]{3,2,1,0:T(8,128)(2,1)S(1)}, u32[]{:S(2)}, u32[]{:S(2)}) collective-permute-start(bf16[3,2,16,640]{3,2,1,0:T(8,128)(2,1)S(1)} %bitcast.218), channel_id=1, source_target_pairs={{0,16},{8,24},{16,0},{24,8},{1,17},{9,25},{17,1},{25,9},{2,18},{10... | collective-permute-start | bytes 368648 | tf_op jit(solution)/shard_map/ppermute | solution.py:36
  7.8 18.0 %collective-permute-start.2 = (bf16[3,2,16,640]{3,2,1,0:T(8,128)(2,1)S(1)}, bf16[3,2,16,640]{3,2,1,0:T(8,128)(2,1)S(1)}, u32[]{:S(2)}, u32[]{:S(2)}) collective-permute-start(bf16[3,2,16,640]{3,2,1,0:T(8,128)(2,1)S(1)} %bitcast.220), channel_id=1, source_target_pairs={{0,24},{8,16},{16,8},{24,0},{1,25},{9,17},{17,9},{25,1},{2,26},{10... | collective-permute-start | bytes 368648 | tf_op jit(solution)/shard_map/ppermute | solution.py:36
  21.0 11.0 %all-to-all-start = ((bf16[4,2,30720]{2,1,0:T(2,128)(2,1)}), bf16[4,2,30720]{2,1,0:T(2,128)(2,1)S(1)}, u32[]{:S(2)}, u32[]{:S(2)}) async-start(bf16[4,2,30720]{2,1,0:T(2,128)(2,1)} %reshape.318), calls=%async_computation | async-start | bytes 983040 | tf_op jit(solution)/shard_map/all_to_all | solution.py:99
  47.2 31.1 %all-to-all-start.1 = ((bf16[3,2,64,640]{3,1,0,2:T(2,128)(2,1)}), bf16[3,2,64,640]{3,1,0,2:T(2,128)(2,1)S(1)}, u32[]{:S(2)}, u32[]{:S(2)}) async-start(bf16[3,2,64,640]{3,1,0,2:T(2,128)(2,1)} %copy.93), calls=%async_computation.1 | async-start | bytes 983040 | tf_op jit(solution)/shard_map/all_to_all | solution.py:108
  79.6 10.1 %copy-start.1 = (bf16[128,16,2560]{2,0,1:T(8,128)(2,1)S(1)}, bf16[128,16,2560]{2,0,1:T(8,128)(2,1)}, u32[]{:S(2)}) copy-start(bf16[128,16,2560]{2,0,1:T(8,128)(2,1)} %gather_fusion.1) | copy-start | bytes 31457284
  89.6 15.4 %copy-start.2 = (bf16[16,128,128]{2,1,0:T(8,128)(2,1)S(1)}, bf16[16,128,128]{2,1,0:T(8,128)(2,1)}, u32[]{:S(2)}) copy-start(bf16[16,128,128]{2,1,0:T(8,128)(2,1)} %param.12) | copy-start | bytes 1572868
  89.6 15.4 %copy-start.3 = (f32[2,16,128]{2,1,0:T(8,128)S(1)}, f32[2,16,128]{2,1,0:T(8,128)}, u32[]{:S(2)}) copy-start(f32[2,16,128]{2,1,0:T(8,128)} %param.14) | copy-start | bytes 49156
